TPU v7x, 32 devices: a whole 2x2x4 slice. The times are simulated.
32 devices in a mesh: row: 4 (over z), col: 8 (over y, x, core).
Axes of the slice: x: 2, y: 2, z: 4, core: 2. Of those that a mesh axis runs over, the one named last changes fastest.
Arguments:
- front_matrix: bfloat16 [32768, 32768], P('row', 'col'), may hold values from -0.03125 to 0.03125
- right_random: bfloat16 [32768, 128], P(('col', 'row')), may hold values from -32 to 32
- left_random: bfloat16 [32768, 128], P(('row', 'col')), may hold values from -32 to 32
- row_basis: bfloat16 [32768, 384], P('row'), may hold values from -1 to 1, as said below
- column_basis: bfloat16 [32768, 384], P('col'), may hold values from -1 to 1, as said below
Outputs:
- row_samples: float32 [128, 32768], P('col', 'row')
- column_samples: float32 [128, 32768], P('row', 'col')
- row_spread: float32 [64], P('row')
- column_spread: float32 [64], P('col')
Inputs may be any that keep to these rules, and one draw needn't show every extreme that they name: Within each leaf node's 512 rows, the columns of row_basis are orthonormal up to their rounding to bfloat16. Within each leaf node's 512 rows, the columns of column_basis are orthonormal up to their rounding to bfloat16.
All inputs are finite; a program needn't handle non-finite values.
Results may differ from a plain program's by a relative error of at most 0.0003.
Values may be sent and summed in bfloat16 or wider, within the bound.
A program may use at most 128 MiB of HBM per device.

v0:
```python
import jax
import jax.numpy as jnp
from jax import lax
from jax.sharding import PartitionSpec as P

SAMPLES = 128
EARLIER = 384
NODE = 512


def project_out(samples, basis):
    count = samples.shape[0]
    nodes = basis.shape[0] // NODE
    shaped = samples.reshape(count, nodes, NODE)
    stacked = basis.astype(jnp.float32).reshape(nodes, NODE, EARLIER)
    coeffs = jnp.einsum("knr,nre->kne", shaped, stacked, precision=lax.Precision.HIGHEST)
    correction = jnp.einsum("kne,nre->knr", coeffs, stacked, precision=lax.Precision.HIGHEST)
    cleaned = shaped - correction
    squares = jnp.sum(cleaned * cleaned, axis=(0, 2))
    return (cleaned.reshape(count, nodes * NODE), squares)


def shards(front_matrix, right_random, left_random, row_basis, column_basis):
    row_partial = jnp.einsum(
        "jc,ij->ci",
        lax.all_gather(right_random, "row", axis=0, tiled=True),
        front_matrix,
        preferred_element_type=jnp.float32,
    )
    column_partial = jnp.einsum(
        "ic,ij->cj",
        lax.all_gather(left_random, "col", axis=0, tiled=True),
        front_matrix,
        preferred_element_type=jnp.float32,
    )
    row_mine = lax.psum_scatter(row_partial, "col", scatter_dimension=0, tiled=True)
    column_mine = lax.psum_scatter(column_partial, "row", scatter_dimension=0, tiled=True)
    row_samples, row_partial_sq = project_out(row_mine, row_basis)
    column_samples, column_partial_sq = project_out(column_mine, column_basis)
    row_total_sq = lax.psum(row_partial_sq, "col")
    column_total_sq = lax.psum(column_partial_sq, "row")
    row_spread = jnp.sqrt(row_total_sq / (SAMPLES * NODE))
    column_spread = jnp.sqrt(column_total_sq / (SAMPLES * NODE))
    return (row_samples, column_samples, row_spread, column_spread)


def solution(mesh):
    in_specs = (
        P("row", "col"),
        P(("col", "row"), None),
        P(("row", "col"), None),
        P("row", None),
        P("col", None),
    )
    out_specs = (P("col", "row"), P("row", "col"), P("row"), P("col"))
    return jax.shard_map(shards, mesh=mesh, in_specs=in_specs, out_specs=out_specs, check_vma=False)
```

profile of v0, /device:TPU:0, one launch (start us, length us, event | category | flops | bytes accessed | tf_op | source)
XLA Modules:
  0.0 207.1 jit_solution(11374009316376437406)
XLA Ops:
  7.2 0.0 all-gather.3.cloned.1.call-start
  7.2 0.7 all-gather.3.cloned.1.call-update
  7.9 0.0 all-gather.5.cloned.1.call-start
  8.0 0.7 all-gather.5.cloned.1.call-update
  8.7 0.0 reduce-scatter.3.cloned.1.call-start
  8.7 31.6 %all-gather.3.cloned.1.call-done = bf16[4096,128]{1,0:T(8,128)(2,1)} async-done(((bf16[1024,128]{1,0:T(8,128)(2,1)}), bf16[4096,128]{1,0:T(8,128)(2,1)}) %all-gather.3.cloned.1.call-update) | async-done | bytes 1048592 | tf_op jit(solution)/shard_map/all_gather | solution.py:26
  40.3 29.5 %fusion.6 = f32[128,8192]{1,0:T(8,128)} fusion(bf16[4096,128]{1,0:T(8,128)(2,1)} %all-gather.3.cloned.1.call-done, bf16[8192,4096]{1,0:T(8,128)(2,1)} %param.5), kind=kOutput, calls=%fused_computation.14 | convolution fusion | flops 8589934592 | bytes 72351744 | tf_op jit(solution)/shard_map/jc,ij->ci/dot_general | solution.py:24
  69.8 0.0 reduce-scatter.3.cloned.1.call-update
  69.8 0.2 reduce-scatter.5.cloned.1.call-start
  70.1 0.0 all-gather.5.cloned.1.call-done
  70.1 27.7 %fusion.7 = f32[128,4096]{1,0:T(8,128)} fusion(bf16[8192,128]{1,0:T(8,128)(2,1)} %all-gather.5.cloned.1.call-done, bf16[8192,4096]{1,0:T(8,128)(2,1)} %param.5), kind=kOutput, calls=%fused_computation.15 | convolution fusion | flops 8589934592 | bytes 71303168 | tf_op jit(solution)/shard_map/ic,ij->cj/dot_general | solution.py:30
  97.7 0.0 reduce-scatter.5.cloned.1.call-update
  97.8 26.1 %reduce-scatter.3.cloned.1.call-done = f32[16,8192]{1,0:T(8,128)} async-done(((f32[128,8192]{1,0:T(8,128)}), f32[16,8192]{1,0:T(8,128)}) %reduce-scatter.3.cloned.1.call-update) | async-done | bytes 524304 | tf_op jit(solution)/shard_map/reduce_scatter | solution.py:36
  123.9 5.6 %convolution_bitcast_fusion.3 = f32[16,16,384]{2,0,1:T(8,128)S(1)} fusion(bf16[16,512,384]{2,1,0:T(8,128)(2,1)} %bitcast.40, f32[2,16,8,512]{3,2,1,0:T(8,128)} %bitcast.45), kind=kOutput, calls=%fused_computation.5 | convolution fusion | flops 603979776 | bytes 7208960 | tf_op jit(solution)/shard_map/knr,nre->kne/dot_general | solution.py:16
  129.5 7.2 %multiply_reduce_fusion.1 = (f32[16]{0:T(128)S(1)}, f32[16,16,512]{2,0,1:T(8,128)S(1)}) fusion(f32[16,16,384]{2,0,1:T(8,128)S(1)} %convolution_bitcast_fusion.3, bf16[16,512,384]{2,1,0:T(8,128)(2,1)} %bitcast.41, f32[2,16,8,512]{3,2,1,0:T(8,128)S(1)} %bitcast.46), kind=kOutput, calls=%fused_computation.9 | convolution fusion | flops 604372992 | bytes 7733312 | tf_op jit(solution)/shard_map/kne,nre->knr/dot_general | solution.py:17
  136.7 0.8 copy.17
  137.5 32.2 %reduce-scatter.5.cloned.1.call-done = f32[32,4096]{1,0:T(8,128)} async-done(((f32[128,4096]{1,0:T(8,128)}), f32[32,4096]{1,0:T(8,128)}) %reduce-scatter.5.cloned.1.call-update) | async-done | bytes 524304 | tf_op jit(solution)/shard_map/reduce_scatter | solution.py:37
  169.7 2.6 %convolution_bitcast_fusion.2 = f32[32,8,384]{2,0,1:T(8,128)S(1)} fusion(bf16[8,512,384]{2,1,0:T(8,128)(2,1)S(1)} %bitcast.38, f32[4,8,8,512]{3,2,1,0:T(8,128)} %bitcast.43), kind=kOutput, calls=%fused_computation.4 | convolution fusion | flops 603979776 | bytes 4063232 | tf_op jit(solution)/shard_map/knr,nre->kne/dot_general | solution.py:16
  172.4 3.0 %multiply_reduce_fusion = (f32[8]{0:T(128)S(1)}, f32[32,8,512]{2,0,1:T(8,128)S(1)}) fusion(f32[32,8,384]{2,0,1:T(8,128)S(1)} %convolution_bitcast_fusion.2, bf16[8,512,384]{2,1,0:T(8,128)(2,1)S(1)} %bitcast.39, f32[4,8,8,512]{3,2,1,0:T(8,128)S(1)} %bitcast.44), kind=kOutput, calls=%fused_computation.8 | convolution fusion | flops 604372992 | bytes 4587552 | tf_op jit(solution)/shard_map/kne,nre->knr/dot_general | solution.py:17
  175.4 0.8 copy.18
  176.2 13.2 %psum.14 = f32[16]{0:T(128)S(1)} all-reduce(f32[16]{0:T(128)S(1)} %get-tuple-element.4), channel_id=1, replica_groups=mesh['row'=4,'col'=8] {'col'}, use_global_device_ids=true, to_apply=%region_3.0 | all-reduce | flops 16 | bytes 128 | tf_op jit(solution)/shard_map/psum | solution.py:40
  189.4 0.5 multiply_sqrt_fusion.1
  189.9 10.2 %psum.15 = f32[8]{0:T(128)S(1)} all-reduce(f32[8]{0:T(128)S(1)} %get-tuple-element.6), channel_id=1, replica_groups=mesh['row'=4,'col'=8] {'row'}, use_global_device_ids=true, to_apply=%region_5.0 | all-reduce | flops 8 | bytes 64 | tf_op jit(solution)/shard_map/psum | solution.py:41
  200.1 0.5 multiply_sqrt_fusion
  (6 shorter events, 0.0 us)
Async XLA Ops:
  7.2 162.6 %copy-start = (bf16[4096,384]{1,0:T(8,128)(2,1)S(1)}, bf16[4096,384]{1,0:T(8,128)(2,1)}, u32[]{:S(2)}) copy-start(bf16[4096,384]{1,0:T(8,128)(2,1)} %param.9) | copy-start | bytes 9437188
  7.2 33.1 %all-gather.3.cloned.1.call-start = ((), (), s32[]{:S(2)}) async-start(), calls=%async_computation.2 | async-start | bytes 1310720 | tf_op jit(solution)/shard_map/all_gather | solution.py:26
  7.9 62.2 %all-gather.5.cloned.1.call-start = ((), (), s32[]{:S(2)}) async-start(), calls=%async_computation.4 | async-start | bytes 2359296 | tf_op jit(solution)/shard_map/all_gather | solution.py:32
  8.7 115.2 %reduce-scatter.3.cloned.1.call-start = ((), (), s32[]{:S(2)}) async-start(), calls=%async_computation.3 | async-start | bytes 4718592 | tf_op jit(solution)/shard_map/reduce_scatter | solution.py:36
  69.8 99.9 %reduce-scatter.5.cloned.1.call-start = ((), (), s32[]{:S(2)}) async-start(), calls=%async_computation.5 | async-start | bytes 2621440 | tf_op jit(solution)/shard_map/reduce_scatter | solution.py:37
  123.9 5.6 %copy-start.2 = (f32[16,8192]{1,0:T(8,128)S(1)}, f32[16,8192]{1,0:T(8,128)}, u32[]{:S(2)}) copy-start(f32[16,8192]{1,0:T(8,128)} %reduce-scatter.3.cloned.1.call-done) | copy-start | bytes 1572868
  169.7 2.6 %copy-start.1 = (f32[32,4096]{1,0:T(8,128)S(1)}, f32[32,4096]{1,0:T(8,128)}, u32[]{:S(2)}) copy-start(f32[32,4096]{1,0:T(8,128)} %reduce-scatter.5.cloned.1.call-done) | copy-start | bytes 1572868
Sparse Core Ops, SparseCore 0:
  9.6 30.6 all-gather.2
  42.2 27.1 all-gather.4
  72.7 51.1 reduce-scatter.2
  126.1 43.6 reduce-scatter.4
where the time goes:
time: 207 us
  waiting for transfers between devices  91.3 us (44%)
  matrix products  75.6 us (37%)
  blocking collectives  23.4 us (11%)
  between operations  13.8 us (7%)
    reduce_scatter x1, waiting for transfers between devices, shards(): lax.psum_scatter(column_partial, 'row', scatter_dimension=0, tiled=True)  32.2 us
    all_gather x1, waiting for transfers between devices, shards(): lax.all_gather(right_random, 'row', axis=0, tiled=True)  31.6 us
    dot_general x1, matrix products, shards(): jnp.einsum('jc,ij->ci', lax.all_gather(right_random, 'row', axis=0, tiled...  29.5 us
    dot_general x1, matrix products, shards(): jnp.einsum('ic,ij->cj', lax.all_gather(left_random, 'col', axis=0, tiled=...  27.7 us
    reduce_scatter x1, waiting for transfers between devices, shards(): lax.psum_scatter(row_partial, 'col', scatter_dimension=0, tiled=True)  26.1 us
    psum x1, blocking collectives, shards(): row_total_sq = lax.psum(row_partial_sq, 'col')  13.2 us
    dot_general x2, matrix products, project_out(): jnp.einsum('kne,nre->knr', coeffs, stacked, precision=lax.Precision.HIGHEST)  10.2 us
    psum x1, blocking collectives, shards(): column_total_sq = lax.psum(column_partial_sq, 'row')  10.2 us
  transfers between devices with their start and end apart: 4, of which 3 were waited for; matrix products, arithmetic and copies ran while one was open for 34% of the time, Pallas kernels for 0%

commit v1 on v0

v1 whole, which is shorter than its diff:
```python
import functools

import jax
import jax.numpy as jnp
from jax import lax
from jax.experimental import pallas as pl
from jax.experimental.pallas import tpu as pltpu
from jax.sharding import PartitionSpec as P

NODE = 512
BUFS = 3
MESH = pl.DeviceIdType.MESH
F32 = jnp.float32
BF16 = jnp.bfloat16


def split3(x):
    hi = x.astype(BF16)
    rest = x - hi.astype(F32)
    mid = rest.astype(BF16)
    lo = (rest - mid.astype(F32)).astype(BF16)
    return hi, mid, lo


def times_basis(x, basis, dims):
    parts = split3(x)
    s = x.shape[0]
    if s % 16 == 0:
        y = lax.dot_general(jnp.concatenate(parts, axis=0), basis, (dims, ((), ())), preferred_element_type=F32)
        return y[:s] + (y[s:2 * s] + y[2 * s:])
    ys = [lax.dot_general(p, basis, (dims, ((), ())), preferred_element_type=F32) for p in parts]
    return ys[0] + (ys[1] + ys[2])


def project(x, basis):
    coeffs = times_basis(x, basis, ((1,), (0,)))
    return x - times_basis(coeffs, basis, ((1,), (1,)))


def kernel(nrow, ncol, front, right, left, rbasis, cbasis,
           row_out, col_out, rspread, cspread,
           leftbuf, rightbuf, cblk, rblk, acc, crecv, stage, precv, rsum, rchip,
           rb, cb, rsq, csq, rsqbuf, csqbuf,
           lsend, lrecv, gsend, grecv, csend, crsem, psend, prsem, xsend, xrsem,
           ssend, srrecv, screcv, local, bsem, cfsem, rfsem):
    r = lax.axis_index("row")
    c = lax.axis_index("col")
    rows, cols = front.shape
    samples = right.shape[1]
    nchip = ncol // 2
    chip, core = lax.div(c, 2), lax.rem(c, 2)
    partner = lax.bitwise_xor(c, 1)
    kb, half = rows // ncol, cols // 2
    steps = 2 * ncol
    panels = rows // NODE
    cnodes = cols // NODE
    sr, sc = samples // ncol, samples // nrow

    def cfetch(i):
        s, h = lax.rem(i, ncol), lax.div(i, ncol)
        k = lax.bitwise_xor(c, s)
        slot = lax.rem(i, BUFS)
        return pltpu.make_async_copy(
            front.at[pl.ds(pl.multiple_of(k * kb, kb), kb), pl.ds(pl.multiple_of(h * half, half), half)],
            cblk.at[slot], cfsem.at[slot])

    def rfetch(p):
        slot = lax.rem(p, BUFS)
        return pltpu.make_async_copy(front.at[pl.ds(pl.multiple_of(p * NODE, NODE), NODE), :], rblk.at[slot], rfsem.at[slot])

    def lcopy(src, slot, dev):
        return pltpu.make_async_remote_copy(src, leftbuf.at[slot], lsend, lrecv.at[slot], device_id={"col": dev}, device_id_type=MESH)

    def gcopy(slot, dev):
        return pltpu.make_async_remote_copy(right, rightbuf.at[slot], gsend, grecv.at[slot], device_id={"row": dev}, device_id_type=MESH)

    def ccopy(h, block, slot, dev):
        return pltpu.make_async_remote_copy(acc.at[h, block], crecv.at[h, slot], csend, crsem.at[h, slot], device_id={"row": dev}, device_id_type=MESH)

    def pcopy(p):
        return pltpu.make_async_remote_copy(stage.at[p, 1 - core], precv.at[p], psend, prsem.at[p], device_id={"col": partner}, device_id_type=MESH)

    def xcopy(p, block, slot, dev):
        return pltpu.make_async_remote_copy(rsum.at[p, block], rchip.at[p, slot], xsend, xrsem.at[p, slot], device_id={"col": dev}, device_id_type=MESH)

    for i in range(BUFS - 1):
        cfetch(jnp.int32(i)).start()
    own_left = pltpu.make_async_copy(left, leftbuf.at[c], local.at[0])
    own_right = pltpu.make_async_copy(right, rightbuf.at[r], local.at[1])
    own_left.start()
    own_right.start()

    barrier = pltpu.get_barrier_semaphore()
    for s in range(1, ncol):
        pl.semaphore_signal(barrier, inc=1, device_id={"col": lax.bitwise_xor(c, s)}, device_id_type=MESH)
    for t in range(1, nrow):
        pl.semaphore_signal(barrier, inc=1, device_id={"row": lax.bitwise_xor(r, t)}, device_id_type=MESH)
    acc[...] = jnp.zeros_like(acc)
    rsq[...] = jnp.zeros_like(rsq)
    csq[...] = jnp.zeros_like(csq)
    pl.semaphore_wait(barrier, ncol - 1 + nrow - 1)

    lcopy(left, c, partner).start()
    for j in range(1, nchip):
        lcopy(left, c, lax.bitwise_xor(c, 2 * j)).start()
    for t in range(1, nrow):
        gcopy(r, lax.bitwise_xor(r, t)).start()
    bases = (pltpu.make_async_copy(rbasis, rb, bsem.at[0]), pltpu.make_async_copy(cbasis, cb, bsem.at[1]))
    own_left.wait()

    @pl.loop(0, steps)
    def _(i):
        s, h = lax.rem(i, ncol), lax.div(i, ncol)
        k = lax.bitwise_xor(c, s)
        slot = lax.rem(i, BUFS)

        @pl.when(i + BUFS - 1 < steps)
        def _():
            cfetch(i + BUFS - 1).start()

        @pl.when(i + BUFS - 1 >= steps)
        def _():
            rfetch(i + BUFS - 1 - steps).start()

        @pl.when(i == ncol)
        def _():
            for b in bases:
                b.start()

        @pl.when((i > 0) & (i < ncol))
        def _():
            lcopy(left, k, partner).wait_recv()

        @pl.when((i > 1) & (i < ncol) & (lax.rem(i, 2) == 0))
        def _():
            lcopy(leftbuf.at[k], k, partner).start()

        cfetch(i).wait()
        lt = leftbuf[k].T
        width = min(NODE, half)
        for n in range(half // width):
            piece = jnp.dot(lt, cblk[slot, :, n * width:(n + 1) * width], preferred_element_type=F32)
            acc[h, :, :, n * width:(n + 1) * width] += piece.reshape(nrow, sc, width)

        @pl.when(s == ncol - 1)
        def _():
            for t in range(1, nrow):
                peer = lax.bitwise_xor(r, t)
                ccopy(h, peer, r, peer).start()

    own_right.wait()
    for t in range(1, nrow):
        gcopy(lax.bitwise_xor(r, t), r).wait_recv()

    def reduce(p):
        pcopy(p).wait_recv()
        both = stage[p, core] + precv[p]
        rsum[p] = both
        for j in range(1, nchip):
            peer = lax.bitwise_xor(chip, j)
            xcopy(p, peer, chip, peer * 2 + core).start()
        rchip[p, chip] = rsum[p, chip]

    @pl.loop(0, panels)
    def _(p):
        slot = lax.rem(p, BUFS)

        @pl.when(p + BUFS - 1 < panels)
        def _():
            rfetch(p + BUFS - 1).start()

        rfetch(p).wait()
        g = rightbuf[...].reshape(cols, samples)
        res = jnp.dot(rblk[slot], g, preferred_element_type=F32).T
        for d in range(ncol):
            stage[p, d % 2, d // 2] = res[d * sr:(d + 1) * sr]
        pcopy(p).start()

        @pl.when(p > 0)
        def _():
            reduce(p - 1)

    reduce(jnp.int32(panels - 1))
    for b in bases:
        b.wait()

    lane = lax.broadcasted_iota(jnp.int32, rsq.shape, 1)
    per = cnodes // 2
    for h in range(2):
        for t in range(1, nrow):
            peer = lax.bitwise_xor(r, t)
            ccopy(h, r, peer, peer).wait_recv()
        crecv[h, r] = acc[h, r]
        for q in range(per):
            n = h * per + q
            x = crecv[h, 0, :, q * NODE:(q + 1) * NODE]
            for t in range(1, nrow):
                x = x + crecv[h, t, :, q * NODE:(q + 1) * NODE]
            y = project(x, cb[n * NODE:(n + 1) * NODE, :])
            col_out[:, n * NODE:(n + 1) * NODE] = y
            csq[...] = jnp.where(lane == n, jnp.sum(y * y), csq[...])
    csqbuf[r] = csq[...]

    def scopy(t):
        peer = lax.bitwise_xor(r, t)
        return pltpu.make_async_remote_copy(csq, csqbuf.at[r], ssend, screcv.at[r], device_id={"row": peer}, device_id_type=MESH)

    for t in range(1, nrow):
        scopy(t).start()

    unroll = 4 if panels % 4 == 0 else 1

    @pl.loop(0, panels // unroll)
    def _(b):
        for u in range(unroll):
            p = b * unroll + u
            for j in range(1, nchip):
                peer = lax.bitwise_xor(chip, j)
                xcopy(p, chip, peer, peer * 2 + core).wait_recv()
        for u in range(unroll):
            p = b * unroll + u
            x = rchip[p, 0]
            for j in range(1, nchip):
                x = x + rchip[p, j]
            where = pl.ds(pl.multiple_of(p * NODE, NODE), NODE)
            y = project(x, rb[where, :])
            row_out[:, where] = y
            rsq[...] = jnp.where(lane == p, jnp.sum(y * y), rsq[...])

    rsqbuf[c] = rsq[...]

    def tcopy(s):
        peer = lax.bitwise_xor(c, s)
        return pltpu.make_async_remote_copy(rsq, rsqbuf.at[c], ssend, srrecv.at[c], device_id={"col": peer}, device_id_type=MESH)

    for s in range(1, ncol):
        tcopy(s).start()

    def wait_slot(src, buf, sems, slot, dev):
        pltpu.make_async_remote_copy(src, buf.at[slot], ssend, sems.at[slot], device_id=dev, device_id_type=MESH).wait_recv()

    lcopy(left, c, partner).wait_send()
    for j in range(1, nchip):
        lcopy(left, c, partner).wait_send()
        lcopy(leftbuf.at[c], c, partner).wait_send()
    for t in range(1, nrow):
        gcopy(r, r).wait_send()
        for h in range(2):
            ccopy(h, r, r, r).wait_send()

    @pl.loop(0, panels)
    def _(p):
        pcopy(p).wait_send()
        for j in range(1, nchip):
            xcopy(p, chip, chip, c).wait_send()

    for t in range(1, nrow):
        peer = lax.bitwise_xor(r, t)
        wait_slot(csq, csqbuf, screcv, peer, {"row": peer})
    for s in range(1, ncol):
        peer = lax.bitwise_xor(c, s)
        wait_slot(rsq, rsqbuf, srrecv, peer, {"col": peer})
    count = samples * NODE
    total = rsqbuf[0]
    for s in range(1, ncol):
        total = total + rsqbuf[s]
    rspread[...] = jnp.sqrt(total / count)
    total = csqbuf[0]
    for t in range(1, nrow):
        total = total + csqbuf[t]
    cspread[...] = jnp.sqrt(total / count)
    for t in range(1, nrow):
        scopy(t).wait_send()
    for s in range(1, ncol):
        tcopy(s).wait_send()


def shards(nrow, ncol, front, right, left, row_basis, column_basis):
    rows, cols = front.shape
    samples = right.shape[1]
    early = row_basis.shape[1]
    nchip = ncol // 2
    sr, sc = samples // ncol, samples // nrow
    panels = rows // NODE
    half = cols // 2
    dma = pltpu.SemaphoreType.DMA
    hbm = pl.BlockSpec(memory_space=pl.ANY)
    vmem = pl.BlockSpec(memory_space=pltpu.VMEM)
    row_s, col_s, rs, cs = pl.pallas_call(
        functools.partial(kernel, nrow, ncol),
        out_shape=(
            jax.ShapeDtypeStruct((sr, rows), F32),
            jax.ShapeDtypeStruct((sc, cols), F32),
            jax.ShapeDtypeStruct((8, 128), F32),
            jax.ShapeDtypeStruct((8, 128), F32),
        ),
        in_specs=[hbm] * 5,
        out_specs=(vmem,) * 4,
        scratch_shapes=[
            pltpu.VMEM((ncol,) + left.shape, BF16),
            pltpu.VMEM((nrow,) + right.shape, BF16),
            pltpu.VMEM((BUFS, rows // ncol, half), BF16),
            pltpu.VMEM((BUFS, NODE, cols), BF16),
            pltpu.VMEM((2, nrow, sc, half), F32),
            pltpu.VMEM((2, nrow, sc, half), F32),
            pltpu.VMEM((panels, 2, nchip, sr, NODE), F32),
            pltpu.VMEM((panels, nchip, sr, NODE), F32),
            pltpu.VMEM((panels, nchip, sr, NODE), F32),
            pltpu.VMEM((panels, nchip, sr, NODE), F32),
            pltpu.VMEM((rows, early), BF16),
            pltpu.VMEM((cols, early), BF16),
            pltpu.VMEM((8, 128), F32),
            pltpu.VMEM((8, 128), F32),
            pltpu.VMEM((ncol, 8, 128), F32),
            pltpu.VMEM((nrow, 8, 128), F32),
            dma, dma((ncol,)), dma, dma((nrow,)), dma, dma((2, nrow)),
            dma, dma((panels,)), dma, dma((panels, nchip)),
            dma, dma((ncol,)), dma((nrow,)), dma((2,)), dma((2,)), dma((BUFS,)), dma((BUFS,)),
        ],
        compiler_params=pltpu.CompilerParams(
            collective_id=0, has_side_effects=True, vmem_limit_bytes=62 * 1024 * 1024
        ),
    )(front, right, left, row_basis, column_basis)
    return row_s, col_s, rs[0, :rows // NODE], cs[0, :cols // NODE]


def solution(mesh):
    in_specs = (
        P("row", "col"),
        P(("col", "row"), None),
        P(("row", "col"), None),
        P("row", None),
        P("col", None),
    )
    out_specs = (P("col", "row"), P("row", "col"), P("row"), P("col"))
    body = functools.partial(shards, mesh.shape["row"], mesh.shape["col"])
    return jax.shard_map(body, mesh=mesh, in_specs=in_specs, out_specs=out_specs, check_vma=False)
```

time: 207 us -> 91.5 us (0.44)
  the two profiles are of different devices: /device:TPU:0 before, /device:TPU:9 now
where the time goes in v1:
time: 91.5 us; the launch traced here: 91.2 us
  Pallas kernels  84.5 us (92%)
  local copies, waits for them, and re-layouts  6.11 us (7%)
    pallas_call x1, Pallas kernels, shards(): pl.pallas_call(functools.partial(kernel, nrow, ncol), out_shape=(jax.Shap...  84.5 us
    unnamed x2, local copies, waits for them, and re-layouts  3.74 us
    squeeze x2, local copies, waits for them, and re-layouts, shards(): return (row_s, col_s, rs[0, :rows // NODE], cs[0, :cols // NODE])  2.37 us

profile of v1, /device:TPU:9, one launch (start us, length us, event | category | flops | bytes accessed | tf_op | source)
XLA Modules:
  0.0 91.2 jit_solution(9602579831010127680)
XLA Ops:
  0.6 84.5 %shard_map.84 = (f32[16,8192]{1,0:T(8,128)}, f32[32,4096]{1,0:T(8,128)}, f32[8,128]{1,0:T(8,128)}, f32[8,128]{1,0:T(8,128)}) custom-call(bf16[8192,4096]{1,0:T(8,128)(2,1)} %front.1, bf16[1024,128]{1,0:T(8,128)(2,1)} %right.1, bf16[1024,128]{1,0:T(8,128)(2,1)} %left.1, bf16[8192,384]{1,0:T(8,128)(2,1)} %rbasis.1, bf16[4096,384]{1,0:T(8,128)(2,1)} %cbasis.1), custom_call_target="tpu_custom_call" | custom-call | tf_op jit(solution)/shard_map/pallas_call | solution.py:289
  85.1 1.2 %slice_bitcast_fusion.1 = f32[16]{0:T(128)} fusion(f32[8,128]{1,0:T(8,128)} %get-tuple-element.10), kind=kLoop, calls=%fused_computation.1 | loop fusion | bytes 128 | tf_op jit(solution)/shard_map/squeeze | solution.py:324
  86.3 1.2 %slice_bitcast_fusion = f32[8]{0:T(128)} fusion(f32[8,128]{1,0:T(8,128)} %get-tuple-element.11), kind=kLoop, calls=%fused_computation | loop fusion | bytes 64 | tf_op jit(solution)/shard_map/squeeze | solution.py:324
  87.5 1.9 %copy.11 = f32[16,8192]{1,0:T(8,128)} copy(f32[16,8192]{1,0:T(8,128)} %get-tuple-element.16) | data formatting | bytes 1048576
  89.4 1.9 %copy.12 = f32[32,4096]{1,0:T(8,128)} copy(f32[32,4096]{1,0:T(8,128)} %get-tuple-element.17) | data formatting | bytes 1048576

commit v2 on v1

--- a/solution.py
+++ b/solution.py
@@ -32,9 +32,9 @@
     return ys[0] + (ys[1] + ys[2])
 
 
-def project(x, basis):
-    coeffs = times_basis(x, basis, ((1,), (0,)))
-    return x - times_basis(coeffs, basis, ((1,), (1,)))
+def project(xs, bases):
+    coeffs = [times_basis(x, b, ((1,), (0,))) for x, b in zip(xs, bases)]
+    return [x - times_basis(k, b, ((1,), (1,))) for x, k, b in zip(xs, coeffs, bases)]
 
 
 def kernel(nrow, ncol, front, right, left, rbasis, cbasis,
@@ -56,8 +56,15 @@
     cnodes = cols // NODE
     sr, sc = samples // ncol, samples // nrow
 
+    def order(i):
+        j = i - 4
+        early = i < 4
+        s = jnp.where(early, lax.div(i, 2), 2 + lax.rem(jnp.maximum(j, 0), ncol - 2))
+        h = jnp.where(early, lax.rem(i, 2), lax.div(jnp.maximum(j, 0), ncol - 2))
+        return s, h
+
     def cfetch(i):
-        s, h = lax.rem(i, ncol), lax.div(i, ncol)
+        s, h = order(i)
         k = lax.bitwise_xor(c, s)
         slot = lax.rem(i, BUFS)
         return pltpu.make_async_copy(
@@ -110,7 +117,7 @@
 
     @pl.loop(0, steps)
     def _(i):
-        s, h = lax.rem(i, ncol), lax.div(i, ncol)
+        s, h = order(i)
         k = lax.bitwise_xor(c, s)
         slot = lax.rem(i, BUFS)
 
@@ -127,11 +134,11 @@
             for b in bases:
                 b.start()
 
-        @pl.when((i > 0) & (i < ncol))
+        @pl.when((h == 0) & (s > 0))
         def _():
             lcopy(left, k, partner).wait_recv()
 
-        @pl.when((i > 1) & (i < ncol) & (lax.rem(i, 2) == 0))
+        @pl.when((h == 0) & (s > 1) & (lax.rem(s, 2) == 0))
         def _():
             lcopy(leftbuf.at[k], k, partner).start()
 
@@ -191,14 +198,18 @@
             peer = lax.bitwise_xor(r, t)
             ccopy(h, r, peer, peer).wait_recv()
         crecv[h, r] = acc[h, r]
+        xs, marks = [], csq[...]
         for q in range(per):
-            n = h * per + q
             x = crecv[h, 0, :, q * NODE:(q + 1) * NODE]
             for t in range(1, nrow):
                 x = x + crecv[h, t, :, q * NODE:(q + 1) * NODE]
-            y = project(x, cb[n * NODE:(n + 1) * NODE, :])
+            xs.append(x)
+        ys = project(xs, [cb[(h * per + q) * NODE:(h * per + q + 1) * NODE, :] for q in range(per)])
+        for q, y in enumerate(ys):
+            n = h * per + q
             col_out[:, n * NODE:(n + 1) * NODE] = y
-            csq[...] = jnp.where(lane == n, jnp.sum(y * y), csq[...])
+            marks = jnp.where(lane == n, jnp.sum(y * y), marks)
+        csq[...] = marks
     csqbuf[r] = csq[...]
 
     def scopy(t):
@@ -217,15 +228,19 @@
             for j in range(1, nchip):
                 peer = lax.bitwise_xor(chip, j)
                 xcopy(p, chip, peer, peer * 2 + core).wait_recv()
+        xs, places, marks = [], [], rsq[...]
         for u in range(unroll):
             p = b * unroll + u
             x = rchip[p, 0]
             for j in range(1, nchip):
                 x = x + rchip[p, j]
-            where = pl.ds(pl.multiple_of(p * NODE, NODE), NODE)
-            y = project(x, rb[where, :])
-            row_out[:, where] = y
-            rsq[...] = jnp.where(lane == p, jnp.sum(y * y), rsq[...])
+            xs.append(x)
+            places.append(pl.ds(pl.multiple_of(p * NODE, NODE), NODE))
+        ys = project(xs, [rb[where, :] for where in places])
+        for u, y in enumerate(ys):
+            row_out[:, places[u]] = y
+            marks = jnp.where(lane == b * unroll + u, jnp.sum(y * y), marks)
+        rsq[...] = marks
 
     rsqbuf[c] = rsq[...]
 

time: 91.5 us -> 89.9 us (0.983)
  Pallas kernels: 84.5 us -> 82.9 us
    pallas_call x1, Pallas kernels: 84.5 us -> 82.9 us  [shards(): pl.pallas_call(functools.partial(kernel, nrow, ncol), out_shape=(jax.Shap...]
where the time goes in v2:
time: 89.9 us; the launch traced here: 89.6 us
  Pallas kernels  82.9 us (92%)
  local copies, waits for them, and re-layouts  6.11 us (7%)
    pallas_call x1, Pallas kernels, shards(): pl.pallas_call(functools.partial(kernel, nrow, ncol), out_shape=(jax.Shap...  82.9 us
    unnamed x2, local copies, waits for them, and re-layouts  3.74 us
    squeeze x2, local copies, waits for them, and re-layouts, shards(): return (row_s, col_s, rs[0, :rows // NODE], cs[0, :cols // NODE])  2.37 us

profile of v2, /device:TPU:9, one launch (start us, length us, event | category | flops | bytes accessed | tf_op | source)
XLA Modules:
  0.0 89.6 jit_solution(9300571533207367152)
XLA Ops:
  0.6 82.9 %shard_map.84 = (f32[16,8192]{1,0:T(8,128)}, f32[32,4096]{1,0:T(8,128)}, f32[8,128]{1,0:T(8,128)}, f32[8,128]{1,0:T(8,128)}) custom-call(bf16[8192,4096]{1,0:T(8,128)(2,1)} %front.1, bf16[1024,128]{1,0:T(8,128)(2,1)} %right.1, bf16[1024,128]{1,0:T(8,128)(2,1)} %left.1, bf16[8192,384]{1,0:T(8,128)(2,1)} %rbasis.1, bf16[4096,384]{1,0:T(8,128)(2,1)} %cbasis.1), custom_call_target="tpu_custom_call" | custom-call | tf_op jit(solution)/shard_map/pallas_call | solution.py:304
  83.5 1.2 %slice_bitcast_fusion.1 = f32[16]{0:T(128)} fusion(f32[8,128]{1,0:T(8,128)} %get-tuple-element.10), kind=kLoop, calls=%fused_computation.1 | loop fusion | bytes 128 | tf_op jit(solution)/shard_map/squeeze | solution.py:339
  84.7 1.2 %slice_bitcast_fusion = f32[8]{0:T(128)} fusion(f32[8,128]{1,0:T(8,128)} %get-tuple-element.11), kind=kLoop, calls=%fused_computation | loop fusion | bytes 64 | tf_op jit(solution)/shard_map/squeeze | solution.py:339
  85.9 1.9 %copy.11 = f32[16,8192]{1,0:T(8,128)} copy(f32[16,8192]{1,0:T(8,128)} %get-tuple-element.16) | data formatting | bytes 1048576
  87.8 1.9 %copy.12 = f32[32,4096]{1,0:T(8,128)} copy(f32[32,4096]{1,0:T(8,128)} %get-tuple-element.17) | data formatting | bytes 1048576
